TPU v7x, 32 devices: a whole 2x2x4 slice. The times are simulated.
32 devices in a mesh: expert: 8 (over z, core), row: 4 (over y, x).
Axes of the slice: x: 2, y: 2, z: 4, core: 2. Of those that a mesh axis runs over, the one named last changes fastest.
Arguments:
- grads: bfloat16 [8, 7168, 2048], P('expert', 'row')
- basis: bfloat16 [8, 7168, 256], P('expert', 'row'), may hold values from -0.0625 to 0.0625
- loads: int32 [8], P('expert'), may hold values from 1 to 1, as said below
- flags: int32 [8], P('expert'), may hold values 0 or 1
Outputs:
- new_basis: float32 [8, 7168, 256], P('expert', 'row')
- rotated: float32 [8, 256, 2048], P('expert', None, 'row')
Inputs may be any that keep to these rules, and one draw needn't show every extreme that they name: Slots 0 to loads[d] - 1 of expert-axis index d are live and hold experts; the others are empty. Some index has all 1 slots live.
All inputs are finite; a program needn't handle non-finite values. No bound on the sum of `flags` on one device may be relied on, other than what follows from the above.
Results may differ from a plain program's by a relative error of at most 0.006.
Values sent between devices are 32-bit elements; how exact they have to be, the bound alone decides.
A program may use at most 64 MiB of HBM per device.

v0:
```python
import jax
import jax.numpy as jnp
from jax import lax
from jax.sharding import PartitionSpec as P

D = 7168
S = 2048


def on_device(grads, basis, loads, flags):
    slot_count = grads.shape[0]
    live_count = loads[0]
    live_mask = jnp.arange(slot_count, dtype=jnp.int32) < live_count
    refresh = jnp.logical_and(live_mask, flags == 1)
    live_cube = live_mask[:, None, None]
    refresh_cube = refresh[:, None, None]
    squares = jnp.sum(jnp.where(live_cube, jnp.square(grads.astype(jnp.float32)), 0.0))
    leader = (lax.axis_index("row") == 0).astype(jnp.float32)
    total_sq, total_live = lax.psum(
        (squares, leader * live_count.astype(jnp.float32)), ("expert", "row")
    )
    norm_scale = lax.rsqrt(total_sq / (total_live * D * S) + 1e-06)
    local_inner = jnp.einsum("cds,cdk->csk", grads, basis, preferred_element_type=jnp.float32)
    inner_sum = jnp.stack([lax.psum(local_inner[0], "row")])
    inner_gram = jnp.einsum("csk,csj->ckj", inner_sum, inner_sum, precision=lax.Precision.HIGHEST)
    inner_half = inner_sum.astype(jnp.bfloat16)
    power_rows = jnp.einsum(
        "cds,csk->cdk", grads, inner_half, preferred_element_type=jnp.float32
    ).astype(jnp.bfloat16)
    projector = jnp.where(refresh_cube, power_rows, basis)
    local_cross = jnp.einsum("cdk,cds->cks", projector, grads, preferred_element_type=jnp.float32)
    identity = jnp.eye(basis.shape[2], dtype=jnp.float32)
    lower_first = jnp.linalg.cholesky(jnp.where(refresh_cube, inner_gram, identity))
    first_rows = lax.linalg.triangular_solve(
        lower_first, power_rows.astype(jnp.float32), left_side=False, lower=True, transpose_a=True
    )
    local_second = jnp.einsum(
        "cdk,cdj->ckj", first_rows, first_rows, precision=lax.Precision.HIGHEST
    )
    gram_again = lax.psum(local_second, "row")
    cross_cols = lax.psum_scatter(local_cross, "row", scatter_dimension=2, tiled=True)
    lower_second = jnp.linalg.cholesky(jnp.where(refresh_cube, gram_again, identity))
    fresh_basis = lax.linalg.triangular_solve(
        lower_second, first_rows, left_side=False, lower=True, transpose_a=True
    )
    half_solved = lax.linalg.triangular_solve(lower_first, cross_cols, left_side=True, lower=True)
    fresh_rot = lax.linalg.triangular_solve(lower_second, half_solved, left_side=True, lower=True)
    new_basis = jnp.where(
        refresh_cube, fresh_basis, jnp.where(live_cube, basis.astype(jnp.float32), 0.0)
    )
    rotated = jnp.where(refresh_cube, fresh_rot, jnp.where(live_cube, cross_cols, 0.0)) * norm_scale
    return (new_basis, rotated)


def solution(mesh):
    placed = (P("expert", "row", None), P("expert", "row", None), P("expert"), P("expert"))
    return jax.shard_map(
        on_device,
        mesh=mesh,
        in_specs=placed,
        out_specs=(P("expert", "row", None), P("expert", None, "row")),
        check_vma=False,
    )
```

profile of v0, /device:TPU:0, one launch (start us, length us, event | category | flops | bytes accessed | tf_op | source)
XLA Modules:
  0.0 307.3 jit_solution(6141670956639925859)
XLA Ops:
  7.2 6.8 %fusion.4 = f32[2048,256]{1,0:T(8,128)} fusion(bf16[1,1792,2048]{2,1,0:T(8,128)(2,1)} %param.9, bf16[1,1792,256]{2,1,0:T(8,128)(2,1)} %param.10), kind=kOutput, calls=%fused_computation.9 | convolution fusion | flops 1879048192 | bytes 10354688 | tf_op jit(solution)/shard_map/cds,cdk->csk/dot_general | solution.py:23
  14.1 1.1 copy-done.2
  15.2 1.1 copy.12
  17.7 68.7 %all-reduce.5.cloned.1.call-done = f32[2048,256]{1,0:T(8,128)} async-done(((f32[2048,256]{1,0:T(8,128)}), f32[2048,256]{1,0:T(8,128)}) %all-reduce.5.cloned.1.call-update) | async-done | bytes 2097168 | tf_op jit(solution)/shard_map/psum | solution.py:24
  86.4 5.7 %convolution_select_fusion = f32[256,256]{0,1:T(8,128)S(1)} fusion(f32[2048,256]{1,0:T(8,128)} %all-reduce.5.cloned.1.call-done, pred[]{:T(512)} %bitcast), kind=kOutput, calls=%fused_computation.32 | convolution fusion | flops 1610809344 | bytes 2359297 | tf_op jit(solution)/shard_map/csk,csj->ckj/dot_general | solution.py:25
  92.3 0.7 copy-done.3
  93.0 11.7 %custom-call.21 = f32[1,128,128]{2,1,0:T(8,128)S(1)} custom-call(f32[1,128,128]{2,1,0:T(8,128)S(1)} %cholesky.191), custom_call_target="Cholesky" | custom-call | tf_op jit(solution)/shard_map/jit(cholesky)/cholesky | solution.py:33
  104.7 9.8 %custom-call.22 = f32[1,1,128,128]{2,3,1,0:T(8,128)S(1)} custom-call(f32[1,1,128,128]{3,2,1,0:T(8,128)S(1)} %get-tuple-element.68), custom_call_target="InvertDiagBlocksLowerTriangular" | custom-call | tf_op jit(solution)/shard_map/jit(cholesky)/cholesky | solution.py:33
  114.6 1.0 bitcast_dynamic-update-slice_fusion.3
  115.6 1.1 fusion.27
  116.7 11.9 %custom-call.23 = f32[1,128,128]{2,1,0:T(8,128)S(1)} custom-call(f32[1,128,128]{2,1,0:T(8,128)S(1)} %fusion.27), custom_call_target="Cholesky" | custom-call | tf_op jit(solution)/shard_map/jit(cholesky)/cholesky | solution.py:33
  128.6 0.7 compare_reduce_fusion.2
  130.7 3.9 %while.8 = (s32[]{:T(128)}, f32[1,256,256]{2,1,0:T(8,128)S(1)}, s32[2,2]{1,0:T(2,128)S(1)}, f32[2,1,128,128]{3,2,1,0:T(8,128)S(1)}, s32[]{:T(128)}) while((s32[]{:T(128)}, f32[1,256,256]{2,1,0:T(8,128)S(1)}, s32[2,2]{1,0:T(2,128)S(1)}, f32[2,1,128,128]{3,2,1,0:T(8,128)S(1)}, s32[]{:T(128)}) %tuple.57), condition=%wide.while_cond, body=%wide.while_body.sunk | while | flops 2 | bytes 131181 | solution.py:34
  130.7 0.6 fusion.71
  131.3 1.4 bitcast_dynamic-update-slice_fusion.6
  132.7 0.6 fusion.71
  133.3 1.4 bitcast_dynamic-update-slice_fusion.6
  134.6 19.7 %custom-call.24 = f32[1,2,128,128]{2,3,1,0:T(8,128)S(1)} custom-call(f32[1,2,128,128]{3,2,1,0:T(8,128)S(1)} %bitcast.221), custom_call_target="InvertDiagBlocksLowerTriangular" | custom-call | tf_op jit(solution)/shard_map/triangular_solve/custom-call.0 | solution.py:34
  154.3 6.2 %fusion.53 = (f32[1,1792,256]{1,2,0:T(8,128)S(1)}, bf16[1,1792,256]{1,2,0:T(8,128)(2,1)}) fusion(bf16[1,1792,2048]{2,1,0:T(8,128)(2,1)} %param.9, f32[2048,256]{1,0:T(8,128)S(1)} %copy-done), kind=kOutput, calls=%fused_computation.99 | convolution fusion | flops 1880489984 | bytes 12189696 | tf_op jit(solution)/shard_map/cds,csk->cdk/dot_general | solution.py:27
  160.5 1.0 fusion.30
  161.5 1.0 fusion.16
  162.5 1.0 convolution_bitcast_fusion.2
  163.4 2.4 fusion.22
  165.9 6.8 %fusion.6 = f32[1,256,2048]{2,1,0:T(8,128)} fusion(bf16[1,1792,2048]{2,1,0:T(8,128)(2,1)} %param.9, bf16[1,1792,256]{1,2,0:T(8,128)(2,1)} %get-tuple-element.70, bf16[1,1792,256]{1,2,0:T(8,128)(2,1)S(1)} %copy.12, pred[]{:T(512)} %bitcast), kind=kOutput, calls=%fused_computation.11 | convolution fusion | flops 1879506944 | bytes 11272193 | tf_op jit(solution)/shard_map/cdk,cds->cks/dot_general | solution.py:31
  172.7 7.5 %select_reduce_fusion = f32[]{:T(128)} fusion(bf16[1,1792,2048]{2,1,0:T(8,128)(2,1)} %param.9, pred[]{:T(512)} %bitcast.40), kind=kLoop, calls=%fused_computation.4 | loop fusion | flops 14680063 | bytes 7340037 | tf_op jit(solution)/shard_map/reduce_sum | solution.py:17
  180.2 39.4 %all-reduce.1 = (f32[]{:T(128)}, f32[]{:T(128)}) all-reduce(f32[]{:T(128)} %select_reduce_fusion, f32[]{:T(128)S(6)} %mul.13), channel_id=1, replica_groups=mesh['expert'=8,'row'=4] {'expert','row'}, use_global_device_ids=true, to_apply=%region_8.12 | all-reduce | flops 2 | bytes 16 | tf_op jit(solution)/shard_map/psum | solution.py:19
  221.0 1.0 convert_select_fusion
  222.1 1.0 fusion.40
  223.1 12.3 %custom-call.25 = f32[1,128,128]{2,1,0:T(8,128)} custom-call(f32[1,128,128]{2,1,0:T(8,128)S(1)} %cholesky.194), custom_call_target="Cholesky" | custom-call | tf_op jit(solution)/shard_map/jit(cholesky)/cholesky | solution.py:42
  235.5 0.9 cholesky.185
  236.3 1.5 select_reduce_fusion.2
  237.8 11.3 %custom-call.26 = f32[1,1,128,128]{2,3,1,0:T(8,128)} custom-call(f32[1,1,128,128]{3,2,1,0:T(8,128)} %get-tuple-element.64), custom_call_target="InvertDiagBlocksLowerTriangular" | custom-call | tf_op jit(solution)/shard_map/jit(cholesky)/cholesky | solution.py:42
  249.1 1.0 bitcast_dynamic-update-slice_fusion.2
  250.2 0.9 fusion.28
  251.1 12.5 %custom-call.27 = f32[1,128,128]{2,1,0:T(8,128)S(1)} custom-call(f32[1,128,128]{2,1,0:T(8,128)} %fusion.28), custom_call_target="Cholesky" | custom-call | tf_op jit(solution)/shard_map/jit(cholesky)/cholesky | solution.py:42
  263.7 0.6 compare_reduce_fusion
  264.3 0.6 compare_reduce_fusion.1
  266.3 4.0 %while.9 = (s32[]{:T(128)}, f32[1,256,256]{2,1,0:T(8,128)S(1)}, s32[2,2]{1,0:T(2,128)S(1)}, f32[2,1,128,128]{3,2,1,0:T(8,128)S(1)}, s32[]{:T(128)}) while((s32[]{:T(128)}, f32[1,256,256]{2,1,0:T(8,128)S(1)}, s32[2,2]{1,0:T(2,128)S(1)}, f32[2,1,128,128]{3,2,1,0:T(8,128)S(1)}, s32[]{:T(128)}) %tuple.69), condition=%wide.while_cond.clone, body=%wide.while_body.clone.sunk | while | flops 2 | bytes 131181 | solution.py:43
  266.9 1.4 bitcast_dynamic-update-slice_fusion.7
  268.9 1.4 bitcast_dynamic-update-slice_fusion.7
  270.3 19.9 %custom-call.28 = f32[1,2,128,128]{2,3,1,0:T(8,128)S(1)} custom-call(f32[1,2,128,128]{3,2,1,0:T(8,128)S(1)} %bitcast.220), custom_call_target="InvertDiagBlocksLowerTriangular" | custom-call | tf_op jit(solution)/shard_map/triangular_solve/custom-call.0 | solution.py:43
  290.2 0.9 fusion.31
  291.2 1.0 fusion.18
  292.1 1.0 convolution_bitcast_fusion
  293.3 1.7 copy.14
  295.0 1.4 fusion.38
  297.3 1.3 fusion.24
  299.5 0.9 fusion.37
  (44 shorter events, 3.8 us)
Async XLA Ops:
  7.2 79.2 %all-reduce.5.cloned.1.call-start = ((), (), s32[]{:S(2)}) async-start(), calls=%async_computation.1 | async-start | bytes 4194304 | tf_op jit(solution)/shard_map/psum | solution.py:24
  14.0 1.2 copy-start.2
  14.1 206.9 %all-reduce.7.cloned.1.call-start = ((), (), s32[]{:S(2)}) async-start(), calls=%async_computation.2 | async-start | bytes 524288 | tf_op jit(solution)/shard_map/psum | solution.py:40
  92.1 62.3 %copy-start = (f32[2048,256]{1,0:T(8,128)S(1)}, f32[2048,256]{1,0:T(8,128)}, u32[]{:S(2)}) copy-start(f32[2048,256]{1,0:T(8,128)} %all-reduce.5.cloned.1.call-done) | copy-start | bytes 6291460
  92.3 0.7 copy-start.3
  154.3 8.1 %copy-start.4 = (f32[1,2,128,128]{2,3,1,0:T(8,128)}, f32[1,2,128,128]{2,3,1,0:T(8,128)S(1)}, u32[]{:S(2)}) copy-start(f32[1,2,128,128]{2,3,1,0:T(8,128)S(1)} %custom-call.24) | copy-start | bytes 393220
  165.8 129.2 %reduce-scatter.2.cloned.1.call-start = ((), (), s32[]{:S(2)}) async-start(), calls=%async_computation.3 | async-start | bytes 2621440 | tf_op jit(solution)/shard_map/reduce_scatter | solution.py:41
  293.3 1.7 copy-start.5
  295.0 4.4 %copy-start.1 = (f32[1,256,512]{2,1,0:T(8,128)S(1)}, f32[1,256,512]{2,1,0:T(8,128)}, u32[]{:S(2)}) copy-start(f32[1,256,512]{2,1,0:T(8,128)} %reduce-scatter.2.cloned.1.call-done) | copy-start | bytes 1572868
Sparse Core Ops, SparseCore 0:
  14.2 72.1 all-reduce.4
  165.9 43.0 all-reduce.6
  211.9 35.2 reduce-scatter.1
where the time goes:
time: 311 us; the launch traced here: 307 us
  other arithmetic  123 us (40%)
  waiting for transfers between devices  68.8 us (22%)
  matrix products  42 us (14%)
  blocking collectives  39.4 us (13%)
  between operations  19.7 us (6%)
  local copies, waits for them, and re-layouts  13.7 us (4%)
    psum x1, waiting for transfers between devices, on_device(): inner_sum = jnp.stack([lax.psum(local_inner[0], 'row')])  68.7 us
    psum x1, blocking collectives, on_device(): lax.psum((squares, leader * live_count.astype(jnp.float32)), ('expert', '...  39.4 us
    another operation x7, other arithmetic, on_device(): jnp.linalg.cholesky(jnp.where(refresh_cube, gram_again, identity))  39 us
    another operation x6, other arithmetic, on_device(): jnp.linalg.cholesky(jnp.where(refresh_cube, inner_gram, identity))  34.1 us
    another operation x2, other arithmetic, on_device(): lax.linalg.triangular_solve(lower_second, first_rows, left_side=False, lo...  20 us
    another operation x3, other arithmetic, on_device(): lax.linalg.triangular_solve(lower_first, power_rows.astype(jnp.float32),...  19.7 us
    reduce_sum x1, other arithmetic, on_device(): jnp.sum(jnp.where(live_cube, jnp.square(grads.astype(jnp.float32)), 0.0))  7.48 us
    dot_general x1, matrix products, on_device(): jnp.einsum('cds,cdk->csk', grads, basis, preferred_element_type=jnp.float32)  6.82 us
  transfers between devices with their start and end apart: 3, of which 1 were waited for; matrix products, arithmetic and copies ran while one was open for 29% of the time, Pallas kernels for 0%

commit v1 on v0

--- a/solution.py
+++ b/solution.py
@@ -17,7 +17,7 @@
     squares = jnp.sum(jnp.where(live_cube, jnp.square(grads.astype(jnp.float32)), 0.0))
     leader = (lax.axis_index("row") == 0).astype(jnp.float32)
     total_sq, total_live = lax.psum(
-        (squares, leader * live_count.astype(jnp.float32)), ("expert", "row")
+        lax.psum((squares, leader * live_count.astype(jnp.float32)), "expert"), "row"
     )
     norm_scale = lax.rsqrt(total_sq / (total_live * D * S) + 1e-06)
     local_inner = jnp.einsum("cds,cdk->csk", grads, basis, preferred_element_type=jnp.float32)

time: 311 us -> 299 us (0.961)
  blocking collectives: 39.4 us -> 26.1 us
    psum x1 -> x2, blocking collectives: 39.4 us -> 26.1 us  [the longest x1 16.6 us: on_device(): lax.psum((squares, leader * live_count.astype(jnp.float32)), 'expert')]
  transfers between devices with their start and end apart: 3 -> 3, of which waited for: 1 -> 2; matrix products, arithmetic and copies ran while one was open for 29% -> 30% of each run, Pallas kernels for 0% -> 0%
where the time goes in v1:
time: 299 us; the launch traced here: 295 us
  other arithmetic  124 us (41%)
  waiting for transfers between devices  70.3 us (24%)
  matrix products  42 us (14%)
  blocking collectives  26.1 us (9%)
  between operations  19.5 us (7%)
  local copies, waits for them, and re-layouts  13.4 us (4%)
    psum x1, waiting for transfers between devices, on_device(): inner_sum = jnp.stack([lax.psum(local_inner[0], 'row')])  69.1 us
    another operation x7, other arithmetic, on_device(): jnp.linalg.cholesky(jnp.where(refresh_cube, gram_again, identity))  39 us
    another operation x6, other arithmetic, on_device(): jnp.linalg.cholesky(jnp.where(refresh_cube, inner_gram, identity))  34.4 us
    another operation x2, other arithmetic, on_device(): lax.linalg.triangular_solve(lower_second, first_rows, left_side=False, lo...  19.9 us
    another operation x3, other arithmetic, on_device(): lax.linalg.triangular_solve(lower_first, power_rows.astype(jnp.float32),...  19.7 us
    psum x1, blocking collectives, on_device(): lax.psum((squares, leader * live_count.astype(jnp.float32)), 'expert')  16.6 us
    psum x1, blocking collectives, on_device(): lax.psum(lax.psum((squares, leader * live_count.astype(jnp.float32)), 'ex...  9.58 us
    reduce_sum x1, other arithmetic, on_device(): jnp.sum(jnp.where(live_cube, jnp.square(grads.astype(jnp.float32)), 0.0))  7.49 us
  transfers between devices with their start and end apart: 3, of which 2 were waited for; matrix products, arithmetic and copies ran while one was open for 30% of the time, Pallas kernels for 0%

profile of v1, /device:TPU:0, one launch (start us, length us, event | category | flops | bytes accessed | tf_op | source)
XLA Modules:
  0.0 295.3 jit_solution(3365604387327791091)
XLA Ops:
  7.2 6.8 %fusion.4 = f32[2048,256]{1,0:T(8,128)} fusion(bf16[1,1792,2048]{2,1,0:T(8,128)(2,1)} %param.9, bf16[1,1792,256]{2,1,0:T(8,128)(2,1)} %param.10), kind=kOutput, calls=%fused_computation.9 | convolution fusion | flops 1879048192 | bytes 10354688 | tf_op jit(solution)/shard_map/cds,cdk->csk/dot_general | solution.py:23
  14.1 1.1 copy-done.2
  15.2 0.8 copy.12
  17.3 69.1 %all-reduce.6.cloned.1.call-done = f32[2048,256]{1,0:T(8,128)} async-done(((f32[2048,256]{1,0:T(8,128)}), f32[2048,256]{1,0:T(8,128)}) %all-reduce.6.cloned.1.call-update) | async-done | bytes 2097168 | tf_op jit(solution)/shard_map/psum | solution.py:24
  86.4 5.7 %convolution_select_fusion = f32[256,256]{0,1:T(8,128)S(1)} fusion(f32[2048,256]{1,0:T(8,128)} %all-reduce.6.cloned.1.call-done, pred[]{:T(512)} %bitcast), kind=kOutput, calls=%fused_computation.32 | convolution fusion | flops 1610809344 | bytes 2359297 | tf_op jit(solution)/shard_map/csk,csj->ckj/dot_general | solution.py:25
  92.3 0.7 copy-done.3
  93.0 11.7 %custom-call.21 = f32[1,128,128]{2,1,0:T(8,128)S(1)} custom-call(f32[1,128,128]{2,1,0:T(8,128)S(1)} %cholesky.191), custom_call_target="Cholesky" | custom-call | tf_op jit(solution)/shard_map/jit(cholesky)/cholesky | solution.py:33
  104.8 9.8 %custom-call.22 = f32[1,1,128,128]{2,3,1,0:T(8,128)S(1)} custom-call(f32[1,1,128,128]{3,2,1,0:T(8,128)S(1)} %get-tuple-element.70), custom_call_target="InvertDiagBlocksLowerTriangular" | custom-call | tf_op jit(solution)/shard_map/jit(cholesky)/cholesky | solution.py:33
  114.6 1.0 bitcast_dynamic-update-slice_fusion.3
  115.7 1.1 fusion.27
  116.8 12.1 %custom-call.23 = f32[1,128,128]{2,1,0:T(8,128)S(1)} custom-call(f32[1,128,128]{2,1,0:T(8,128)S(1)} %fusion.27), custom_call_target="Cholesky" | custom-call | tf_op jit(solution)/shard_map/jit(cholesky)/cholesky | solution.py:33
  128.9 0.7 compare_reduce_fusion.2
  130.9 3.9 %while.8 = (s32[]{:T(128)}, f32[1,256,256]{2,1,0:T(8,128)S(1)}, s32[2,2]{1,0:T(2,128)S(1)}, f32[2,1,128,128]{3,2,1,0:T(8,128)S(1)}, s32[]{:T(128)}) while((s32[]{:T(128)}, f32[1,256,256]{2,1,0:T(8,128)S(1)}, s32[2,2]{1,0:T(2,128)S(1)}, f32[2,1,128,128]{3,2,1,0:T(8,128)S(1)}, s32[]{:T(128)}) %tuple.57), condition=%wide.while_cond, body=%wide.while_body.sunk | while | flops 2 | bytes 131181 | solution.py:34
  131.6 1.4 bitcast_dynamic-update-slice_fusion.6
  133.5 1.4 bitcast_dynamic-update-slice_fusion.6
  134.9 19.7 %custom-call.24 = f32[1,2,128,128]{2,3,1,0:T(8,128)S(1)} custom-call(f32[1,2,128,128]{3,2,1,0:T(8,128)S(1)} %bitcast.221), custom_call_target="InvertDiagBlocksLowerTriangular" | custom-call | tf_op jit(solution)/shard_map/triangular_solve/custom-call.0 | solution.py:34
  154.6 6.2 %fusion.53 = (f32[1,1792,256]{1,2,0:T(8,128)S(1)}, bf16[1,1792,256]{1,2,0:T(8,128)(2,1)}) fusion(bf16[1,1792,2048]{2,1,0:T(8,128)(2,1)} %param.9, f32[2048,256]{1,0:T(8,128)S(1)} %copy-done), kind=kOutput, calls=%fused_computation.99 | convolution fusion | flops 1880489984 | bytes 12189696 | tf_op jit(solution)/shard_map/cds,csk->cdk/dot_general | solution.py:27
  160.8 1.0 fusion.30
  161.7 1.0 fusion.16
  162.7 1.0 convolution_bitcast_fusion.2
  163.7 2.4 fusion.22
  166.3 6.8 %fusion.6 = f32[1,256,2048]{2,1,0:T(8,128)} fusion(bf16[1,1792,2048]{2,1,0:T(8,128)(2,1)} %param.9, bf16[1,1792,256]{1,2,0:T(8,128)(2,1)} %get-tuple-element.72, bf16[1,1792,256]{1,2,0:T(8,128)(2,1)S(1)} %copy.12, pred[]{:T(512)} %bitcast), kind=kOutput, calls=%fused_computation.11 | convolution fusion | flops 1879506944 | bytes 11272193 | tf_op jit(solution)/shard_map/cdk,cds->cks/dot_general | solution.py:31
  173.1 7.5 %select_reduce_fusion = f32[]{:T(128)} fusion(bf16[1,1792,2048]{2,1,0:T(8,128)(2,1)} %param.9, pred[]{:T(512)} %bitcast.40), kind=kLoop, calls=%fused_computation.4 | loop fusion | flops 14680063 | bytes 7340037 | tf_op jit(solution)/shard_map/reduce_sum | solution.py:17
  180.6 16.6 %all-reduce.1 = (f32[]{:T(128)}, f32[]{:T(128)}) all-reduce(f32[]{:T(128)} %select_reduce_fusion, f32[]{:T(128)S(6)} %mul.13), channel_id=1, replica_groups=mesh['expert'=8,'row'=4] {'expert'}, use_global_device_ids=true, to_apply=%region_8.12 | all-reduce | flops 2 | bytes 16 | tf_op jit(solution)/shard_map/psum | solution.py:20
  197.2 9.6 %all-reduce.2 = (f32[]{:T(128)}, f32[]{:T(128)}) all-reduce(f32[]{:T(128)} %get-tuple-element.55, f32[]{:T(128)} %get-tuple-element.56), channel_id=1, replica_groups=mesh['expert'=8,'row'=4] {'row'}, use_global_device_ids=true, to_apply=%region_9.13 | all-reduce | flops 2 | bytes 16 | tf_op jit(solution)/shard_map/psum | solution.py:19
  208.1 1.2 all-reduce.8.cloned.1.call-done
  209.3 1.0 convert_select_fusion
  210.4 1.0 fusion.40
  211.4 12.3 %custom-call.25 = f32[1,128,128]{2,1,0:T(8,128)} custom-call(f32[1,128,128]{2,1,0:T(8,128)S(1)} %cholesky.194), custom_call_target="Cholesky" | custom-call | tf_op jit(solution)/shard_map/jit(cholesky)/cholesky | solution.py:42
  223.7 0.9 cholesky.185
  224.6 1.5 select_reduce_fusion.2
  226.1 11.3 %custom-call.26 = f32[1,1,128,128]{2,3,1,0:T(8,128)} custom-call(f32[1,1,128,128]{3,2,1,0:T(8,128)} %get-tuple-element.66), custom_call_target="InvertDiagBlocksLowerTriangular" | custom-call | tf_op jit(solution)/shard_map/jit(cholesky)/cholesky | solution.py:42
  237.4 1.0 bitcast_dynamic-update-slice_fusion.2
  238.4 0.9 fusion.28
  239.3 12.5 %custom-call.27 = f32[1,128,128]{2,1,0:T(8,128)S(1)} custom-call(f32[1,128,128]{2,1,0:T(8,128)} %fusion.28), custom_call_target="Cholesky" | custom-call | tf_op jit(solution)/shard_map/jit(cholesky)/cholesky | solution.py:42
  251.9 0.6 compare_reduce_fusion
  252.6 0.6 compare_reduce_fusion.1
  254.6 4.0 %while.9 = (s32[]{:T(128)}, f32[1,256,256]{2,1,0:T(8,128)S(1)}, s32[2,2]{1,0:T(2,128)S(1)}, f32[2,1,128,128]{3,2,1,0:T(8,128)S(1)}, s32[]{:T(128)}) while((s32[]{:T(128)}, f32[1,256,256]{2,1,0:T(8,128)S(1)}, s32[2,2]{1,0:T(2,128)S(1)}, f32[2,1,128,128]{3,2,1,0:T(8,128)S(1)}, s32[]{:T(128)}) %tuple.69), condition=%wide.while_cond.clone, body=%wide.while_body.clone.sunk | while | flops 2 | bytes 131181 | solution.py:43
  255.2 1.4 bitcast_dynamic-update-slice_fusion.7
  257.2 1.4 bitcast_dynamic-update-slice_fusion.7
  258.6 19.9 %custom-call.28 = f32[1,2,128,128]{2,3,1,0:T(8,128)S(1)} custom-call(f32[1,2,128,128]{3,2,1,0:T(8,128)S(1)} %bitcast.220), custom_call_target="InvertDiagBlocksLowerTriangular" | custom-call | tf_op jit(solution)/shard_map/triangular_solve/custom-call.0 | solution.py:43
  278.5 0.9 fusion.31
  279.4 1.0 fusion.18
  280.4 1.0 convolution_bitcast_fusion
  281.6 1.7 copy.14
  283.2 1.4 fusion.38
  285.5 1.3 fusion.24
  287.7 0.9 fusion.37
  (45 shorter events, 5.1 us)
Async XLA Ops:
  7.2 79.3 %all-reduce.6.cloned.1.call-start = ((), (), s32[]{:S(2)}) async-start(), calls=%async_computation.1 | async-start | bytes 4194304 | tf_op jit(solution)/shard_map/psum | solution.py:24
  14.0 1.2 copy-start.2
  14.1 195.2 %all-reduce.8.cloned.1.call-start = ((), (), s32[]{:S(2)}) async-start(), calls=%async_computation.2 | async-start | bytes 524288 | tf_op jit(solution)/shard_map/psum | solution.py:40
  92.1 62.5 %copy-start = (f32[2048,256]{1,0:T(8,128)S(1)}, f32[2048,256]{1,0:T(8,128)}, u32[]{:S(2)}) copy-start(f32[2048,256]{1,0:T(8,128)} %all-reduce.6.cloned.1.call-done) | copy-start | bytes 6291460
  92.3 0.7 copy-start.3
  154.6 8.1 %copy-start.4 = (f32[1,2,128,128]{2,3,1,0:T(8,128)}, f32[1,2,128,128]{2,3,1,0:T(8,128)S(1)}, u32[]{:S(2)}) copy-start(f32[1,2,128,128]{2,3,1,0:T(8,128)S(1)} %custom-call.24) | copy-start | bytes 393220
  166.1 117.2 %reduce-scatter.2.cloned.1.call-start = ((), (), s32[]{:S(2)}) async-start(), calls=%async_computation.3 | async-start | bytes 2621440 | tf_op jit(solution)/shard_map/reduce_scatter | solution.py:41
  281.5 1.7 copy-start.5
  283.2 4.4 %copy-start.1 = (f32[1,256,512]{2,1,0:T(8,128)S(1)}, f32[1,256,512]{2,1,0:T(8,128)}, u32[]{:S(2)}) copy-start(f32[1,256,512]{2,1,0:T(8,128)} %reduce-scatter.2.cloned.1.call-done) | copy-start | bytes 1572868
Sparse Core Ops, SparseCore 0:
  14.2 72.1 all-reduce.5
  166.2 43.0 all-reduce.7
  212.2 35.3 reduce-scatter.1
